TPU v7x, 64 devices: a 2x2x8 block of a 4x4x8 slice. The times are simulated.
64 devices in a mesh: dp: 4 (over x, y), tp: 16 (over z, core).
Axes of the slice: x: 2, y: 2, z: 8, core: 2. Of those that a mesh axis runs over, the one named last changes fastest.
The devices are a block of a 4x4x8 slice.
Arguments:
- hidden: bfloat16 [4, 4096, 3072], P('dp', 'tp'), parts along dimension 0
- ln1_gain: float32 [3072], replicated
- ln1_bias: float32 [3072], replicated
- w_qkv: bfloat16 [3072, 3, 32, 96], P(None, None, 'tp')
- b_qkv: bfloat16 [3, 32, 96], P(None, 'tp')
- w_out: bfloat16 [32, 96, 3072], P('tp')
- b_out: bfloat16 [3072], replicated
- ln2_gain: float32 [3072], replicated
- ln2_bias: float32 [3072], replicated
- w_up: bfloat16 [3072, 12288], P(None, 'tp')
- b_up: bfloat16 [12288], P('tp')
- w_down: bfloat16 [12288, 3072], P('tp')
- b_down: bfloat16 [3072], replicated
Outputs:
- output: bfloat16 [4, 4096, 3072], P('dp', 'tp'), parts along dimension 0
There are 4 independent parts. A program takes and returns all parts, laid end to end along the dimension named above; an argument that names none is the same for every part.
All inputs are finite; a program needn't handle non-finite values.
Results may differ from a plain program's by a relative error of at most 0.0105452.
Values are sent between devices in bfloat16 or wider.
A program may use at most 768 MiB of HBM per device.

v0:
```python
import jax
import jax.numpy as jnp
from jax import lax
from jax.sharding import PartitionSpec as P

LN_EPS = 1e-5


def layer_norm(inputs, gain_vec, shift_vec):
    as_f32 = inputs.astype(jnp.float32)
    row_mean = jnp.mean(as_f32, axis=-1, keepdims=True)
    centered = as_f32 - row_mean
    variance = jnp.mean(centered * centered, axis=-1, keepdims=True)
    return (centered * lax.rsqrt(variance + LN_EPS) * gain_vec + shift_vec).astype(jnp.bfloat16)


def causal_attention(queries, keys_all, values):
    seq_len = queries.shape[1]
    head_dim = queries.shape[3]
    logits = jnp.einsum("bqhd,bkhd->bhqk", queries, keys_all, preferred_element_type=jnp.float32) * head_dim ** -0.5
    causal = lax.broadcasted_iota(jnp.int32, (seq_len, seq_len), 0) >= lax.broadcasted_iota(jnp.int32, (seq_len, seq_len), 1)
    logits = jnp.where(causal, logits, -1e30)
    row_max = jnp.max(logits, axis=-1, keepdims=True)
    exp_vals = jnp.exp(logits - row_max)
    weights_bf = (exp_vals / jnp.sum(exp_vals, axis=-1, keepdims=True)).astype(jnp.bfloat16)
    return jnp.einsum("bhqk,bkhd->bqhd", weights_bf, values, preferred_element_type=jnp.float32).astype(jnp.bfloat16)


def solution(mesh):
    group_size = mesh.shape["tp"]

    def scatter_sum(partial):
        n_batch, seq_len, feat_dim = partial.shape
        split_view = partial.astype(jnp.bfloat16).reshape(n_batch, group_size, seq_len // group_size, feat_dim)
        received = lax.all_to_all(split_view, "tp", 1, 1, tiled=True)
        return jnp.sum(received.astype(jnp.float32), axis=1)

    def device_body(hidden, ln1_gain, ln1_bias, w_qkv, b_qkv, w_out, b_out, ln2_gain, ln2_bias, w_up, b_up, w_down, b_down):
        normed = layer_norm(hidden, ln1_gain, ln1_bias)
        normed_all = lax.all_gather(normed, "tp", axis=1, tiled=True)
        qkv_acc = jnp.einsum("bsd,dthe->bsthe", normed_all, w_qkv, preferred_element_type=jnp.float32)
        qkv_all = (qkv_acc + b_qkv.astype(jnp.float32)).astype(jnp.bfloat16)
        context = causal_attention(qkv_all[:, :, 0], qkv_all[:, :, 1], qkv_all[:, :, 2])
        attn_part = jnp.einsum("bqhd,hde->bqe", context, w_out, preferred_element_type=jnp.float32)
        attn_sum = scatter_sum(attn_part)
        resid_mid = (hidden.astype(jnp.float32) + (attn_sum + b_out.astype(jnp.float32))).astype(jnp.bfloat16)
        normed_mid = layer_norm(resid_mid, ln2_gain, ln2_bias)
        mid_all = lax.all_gather(normed_mid, "tp", axis=1, tiled=True)
        up_proj = jnp.einsum("bsd,df->bsf", mid_all, w_up, preferred_element_type=jnp.float32) + b_up.astype(jnp.float32)
        gelu_out = jax.nn.gelu(up_proj, approximate=True).astype(jnp.bfloat16)
        down_part = jnp.einsum("bsf,fd->bsd", gelu_out, w_down, preferred_element_type=jnp.float32)
        down_sum = scatter_sum(down_part)
        return (resid_mid.astype(jnp.float32) + (down_sum + b_down.astype(jnp.float32))).astype(jnp.bfloat16)

    in_layout = (P("dp", "tp", None), P(), P(), P(None, None, "tp", None), P(None, "tp", None), P("tp", None, None), P(), P(), P(), P(None, "tp"), P("tp"), P("tp", None), P())
    layer_fn = jax.shard_map(device_body, mesh=mesh, in_specs=in_layout, out_specs=P("dp", "tp", None), check_vma=False)
    return layer_fn
```

profile of v0, /device:TPU:21, one launch (start us, length us, event | category | flops | bytes accessed | tf_op | source)
XLA Modules:
  0.0 1666.5 jit_solution(15706176999231585892)
XLA Ops:
  6.5 0.0 copy-start
  6.6 0.0 copy-start.11
  6.6 0.0 all-gather.3.cloned.1.call-start
  6.6 1.9 convert_reduce_fusion.3
  8.4 2.0 fusion.40
  10.4 3.4 fusion.43
  13.7 0.1 all-gather.3.cloned.1.call-update
  13.8 0.0 copy-done.11
  13.8 11.0 iota_compare_fusion
  24.9 125.6 %all-gather.3.cloned.1.call-done = bf16[1,4096,3072]{2,1,0:T(8,128)(2,1)} async-done(((bf16[1,256,3072]{2,1,0:T(8,128)(2,1)}), bf16[1,4096,3072]{2,1,0:T(8,128)(2,1)}) %all-gather.3.cloned.1.call-update) | async-done | bytes 25165840 | tf_op jit(solution)/shard_map/all_gather | solution.py:40
  150.5 0.0 copy-done
  150.5 18.2 %fusion.8 = f32[4096,576]{0,1:S(1)} fusion(bf16[3072,576]{0,1:T(8,128)(2,1)S(1)} %bitcast.86, bf16[1,4096,3072]{2,1,0:T(8,128)(2,1)} %all-gather.3.cloned.1.call-done), kind=kOutput, calls=%fused_computation.15 | convolution fusion | flops 14495514624 | bytes 38141952
  168.7 3.5 fusion.31
  172.2 67.5 %fusion.54 = (f32[2,4096]{1,0:T(2,128)S(1)}, f32[2,4096,4096]{1,2,0:T(8,128)}) fusion(pred[4096,4096]{0,1:T(8,128)(4,1)} %iota_compare_fusion, bf16[1,4096,3,2,96]{1,4,3,2,0:T(8,128)(2,1)} %fusion.31), kind=kOutput, calls=%fused_computation.73 | convolution fusion | flops 6576672768 | bytes 154173440 | tf_op jit(solution)/shard_map/sub | solution.py:24
  239.7 0.0 copy-start.5
  239.7 43.0 %fusion.30.clone.4 = bf16[4096,2,96]{0,2,1:T(8,128)(2,1)S(1)} fusion(f32[2,4096,4096]{1,2,0:T(8,128)} %get-tuple-element.8, f32[2,4096]{1,0:T(2,128)S(1)} %get-tuple-element.7, bf16[1,4096,3,2,96]{1,4,3,2,0:T(8,128)(2,1)} %fusion.31), kind=kOutput, calls=%fused_computation.35.clone.clone.clone.1 | convolution fusion | flops 6510346240 | bytes 137396224 | tf_op jit(solution)/shard_map/bhqk,bkhd->bqhd/dot_general | solution.py:26
  282.7 0.0 copy-done.5
  282.7 11.7 bitcast_convert_fusion
  294.5 0.0 copy-start.8
  294.5 5.8 all-to-all-start
  300.2 0.1 all-gather.5.cloned.1.call-start
  300.3 0.0 copy-done.8
  300.3 0.0 copy-start.2
  300.3 569.2 %all-to-all-done = bf16[1,16,256,3072]{3,2,0,1:T(8,128)(2,1)} async-done(((bf16[1,16,256,3072]{3,2,0,1:T(8,128)(2,1)}), bf16[1,16,256,3072]{3,2,0,1:T(8,128)(2,1)}, u32[]{:S(2)}, u32[]{:S(2)}) %all-to-all-start) | async-done | bytes 25165856 | tf_op jit(solution)/shard_map/all_to_all | solution.py:35
  869.6 13.7 convert_reduce_fusion.1
  883.3 0.0 copy-done.2
  883.3 0.0 copy-start.6
  883.3 0.0 copy-start.7
  883.3 0.7 convert_reduce_fusion.2
  884.0 0.0 copy-start.3
  884.0 0.0 copy-start.10
  884.0 0.6 fusion.36
  884.6 0.0 copy-done.6
  884.6 0.0 copy-done.7
  884.6 2.0 fusion.39
  886.6 0.1 all-gather.5.cloned.1.call-update
  886.7 0.0 copy-done.10
  886.7 130.1 %all-gather.5.cloned.1.call-done = bf16[1,4096,3072]{2,1,0:T(8,128)(2,1)} async-done(((bf16[1,256,3072]{2,1,0:T(8,128)(2,1)}), bf16[1,4096,3072]{2,1,0:T(8,128)(2,1)}) %all-gather.5.cloned.1.call-update) | async-done | bytes 25165840 | tf_op jit(solution)/shard_map/all_gather | solution.py:48
  1016.8 26.6 %fusion.19.clone.4 = bf16[4096,768]{1,0:T(8,128)(2,1)S(1)} fusion(bf16[3072,768]{1,0:T(8,128)(2,1)} %param.22, bf16[1,4096,3072]{2,1,0:T(8,128)(2,1)} %all-gather.5.cloned.1.call-done, f32[768]{0:T(1024)S(1)} %convert_element_type.84), kind=kOutput, calls=%fused_computation.27.clone.clone.clone.1 | convolution fusion | flops 19358810112 | bytes 36178944 | tf_op jit(solution)/shard_map/bsd,df->bsf/dot_general | solution.py:49
  1043.4 0.0 copy-done.3
  1043.4 25.2 %convolution_convert_fusion = bf16[4096,3072]{1,0:T(8,128)(2,1)} fusion(bf16[768,3072]{1,0:T(8,128)(2,1)} %param.24, bf16[4096,768]{1,0:T(8,128)(2,1)S(1)} %fusion.19.clone.4), kind=kOutput, calls=%fused_computation.17 | convolution fusion | flops 19339935744 | bytes 36175872 | tf_op jit(solution)/shard_map/bsf,fd->bsd/dot_general | solution.py:51
  1068.6 0.0 copy-start.9
  1068.6 5.8 all-to-all-start.1
  1074.4 0.0 copy-done.9
  1074.5 569.3 %all-to-all-done.1 = bf16[1,16,256,3072]{3,2,0,1:T(8,128)(2,1)} async-done(((bf16[1,16,256,3072]{3,2,0,1:T(8,128)(2,1)}), bf16[1,16,256,3072]{3,2,0,1:T(8,128)(2,1)}, u32[]{:S(2)}, u32[]{:S(2)}) %all-to-all-start.1) | async-done | bytes 25165856 | tf_op jit(solution)/shard_map/all_to_all | solution.py:35
  1643.7 0.0 copy-start.4
  1643.8 0.0 copy-start.1
  1643.8 14.2 convert_reduce_fusion
  1658.0 0.0 copy-done.4
  1658.0 1.6 fusion.45
  1659.6 0.0 copy-done.1
  (8 shorter events, 0.0 us)
Async XLA Ops:
  6.5 143.9 %copy-start = (bf16[3072,3,2,96]{0,3,2,1:T(8,128)(2,1)S(1)}, bf16[3072,3,2,96]{0,3,2,1:T(8,128)(2,1)}, u32[]{:S(2)}) copy-start(bf16[3072,3,2,96]{0,3,2,1:T(8,128)(2,1)} %param.16) | copy-start | bytes 10616836
  6.6 7.3 copy-start.11
  6.6 143.9 %all-gather.3.cloned.1.call-start = ((), (), s32[]{:S(2)}) async-start(), calls=%async_computation.2 | async-start | bytes 26738688 | tf_op jit(solution)/shard_map/all_gather | solution.py:40
  239.7 43.0 %copy-start.5 = (bf16[2,96,3072]{2,1,0:T(8,128)(2,1)S(1)}, bf16[2,96,3072]{2,1,0:T(8,128)(2,1)}, u32[]{:S(2)}) copy-start(bf16[2,96,3072]{2,1,0:T(8,128)(2,1)} %param.18) | copy-start | bytes 3538948
  294.5 5.9 copy-start.8
  294.5 575.1 %all-to-all-start = ((bf16[1,16,256,3072]{3,2,0,1:T(8,128)(2,1)}), bf16[1,16,256,3072]{3,2,0,1:T(8,128)(2,1)}, u32[]{:S(2)}, u32[]{:S(2)}) async-start(bf16[1,16,256,3072]{3,2,0,1:T(8,128)(2,1)} %bitcast.87), calls=%async_computation | async-start | bytes 50331648 | tf_op jit(solution)/shard_map/all_to_all | solution.py:35
  300.2 716.6 %all-gather.5.cloned.1.call-start = ((), (), s32[]{:S(2)}) async-start(), calls=%async_computation.3 | async-start | bytes 26738688 | tf_op jit(solution)/shard_map/all_gather | solution.py:48
  300.3 583.0 %copy-start.2 = (bf16[1,256,3072]{2,1,0:T(8,128)(2,1)S(1)}, bf16[1,256,3072]{2,1,0:T(8,128)(2,1)}, u32[]{:S(2)}) copy-start(bf16[1,256,3072]{2,1,0:T(8,128)(2,1)} %param.13) | copy-start | bytes 4718596
  883.3 1.3 copy-start.6
  883.3 1.3 copy-start.7
  884.0 159.4 %copy-start.3 = (bf16[1,256,3072]{2,1,0:T(8,128)(2,1)}, bf16[1,256,3072]{2,1,0:T(8,128)(2,1)S(1)}, u32[]{:S(2)}) copy-start(bf16[1,256,3072]{2,1,0:T(8,128)(2,1)S(1)} %get-tuple-element.6) | copy-start | bytes 4718596
  884.0 2.7 copy-start.10
  1068.6 5.8 copy-start.9
  1068.6 575.1 %all-to-all-start.1 = ((bf16[1,16,256,3072]{3,2,0,1:T(8,128)(2,1)}), bf16[1,16,256,3072]{3,2,0,1:T(8,128)(2,1)}, u32[]{:S(2)}, u32[]{:S(2)}) async-start(bf16[1,16,256,3072]{3,2,0,1:T(8,128)(2,1)} %bitcast.88), calls=%async_computation.1 | async-start | bytes 50331648 | tf_op jit(solution)/shard_map/all_to_all | solution.py:35
  1643.7 14.2 copy-start.4
  1643.8 15.9 copy-start.1
Sparse Core Ops, SparseCore 0:
  13.9 136.5 all-gather.2
  886.8 129.9 all-gather.4
where the time goes:
time: 1670 us
  waiting for transfers between devices  1390 us (83%)
  matrix products  192 us (11%)
  other arithmetic  54.5 us (3%)
    all_to_all x2, waiting for transfers between devices, scatter_sum(): received = lax.all_to_all(split_view, 'tp', 1, 1, tiled=True)  1140 us
    all_gather x1, waiting for transfers between devices, device_body(): mid_all = lax.all_gather(normed_mid, 'tp', axis=1, tiled=True)  130 us
    all_gather x1, waiting for transfers between devices, device_body(): normed_all = lax.all_gather(normed, 'tp', axis=1, tiled=True)  126 us
    sub x1, matrix products, causal_attention(): exp_vals = jnp.exp(logits - row_max)  67.5 us
    dot_general x1, matrix products, causal_attention(): jnp.einsum('bhqk,bkhd->bqhd', weights_bf, values, preferred_element_type=...  43 us
  transfers between devices with their start and end apart: 4, of which 4 were waited for; matrix products, arithmetic and copies ran while one was open for 1% of the time, Pallas kernels for 0%

commit v1 on v0

v1 whole, which is shorter than its diff:
```python
import functools
import math

import jax
import jax.numpy as jnp
from jax import lax
from jax.experimental import pallas as pl
from jax.experimental.pallas import tpu as pltpu
from jax.sharding import PartitionSpec as P

LN_EPS = 1e-5
LANES = 128
MESH_IDS = pl.DeviceIdType.MESH


def layer_norm(inputs, gain_vec, shift_vec):
    as_f32 = inputs.astype(jnp.float32)
    row_mean = jnp.mean(as_f32, axis=-1, keepdims=True)
    centered = as_f32 - row_mean
    variance = jnp.mean(centered * centered, axis=-1, keepdims=True)
    return (centered * lax.rsqrt(variance + LN_EPS) * gain_vec + shift_vec).astype(jnp.bfloat16)


def attention_kernel(blk, scale, q_ref, k_ref, v_ref, o_ref):
    n_heads, seq, width = q_ref.shape
    factor = scale * math.log2(math.e)
    row = lax.broadcasted_iota(jnp.int32, (blk, blk), 0)
    col = lax.broadcasted_iota(jnp.int32, (blk, blk), 1)

    def block(queries, j, carry, masked):
        out = []
        for h in range(n_heads):
            m, l, acc = carry[h]
            rows = pl.ds(pl.multiple_of(j * blk, blk), blk)
            s = lax.dot_general(queries[h], k_ref[h, rows, :], (((1,), (1,)), ((), ())),
                                preferred_element_type=jnp.float32)
            if masked:
                s = jnp.where(row >= col, s, -1e30)
            m_new = jnp.maximum(m, jnp.max(s, axis=-1, keepdims=True))
            p = jnp.exp2((s - m_new) * factor)
            alpha = jnp.exp2((m - m_new) * factor)
            l = l * alpha + jnp.sum(p, axis=-1, keepdims=True)
            acc = acc * alpha + jnp.dot(p.astype(jnp.bfloat16), v_ref[h, rows, :],
                                        preferred_element_type=jnp.float32)
            out.append((m_new, l, acc))
        return tuple(out)

    def per_block(i, _):
        rows = pl.ds(pl.multiple_of(i * blk, blk), blk)
        queries = [q_ref[h, rows, :] for h in range(n_heads)]
        init = tuple(
            (jnp.full((blk, 1), -1e30, jnp.float32), jnp.zeros((blk, 1), jnp.float32),
             jnp.zeros((blk, width), jnp.float32)) for _ in range(n_heads))
        carry = block(queries, i, init, True)
        carry = lax.fori_loop(0, i, lambda j, c: block(queries, j, c, False), carry)
        for h in range(n_heads):
            o_ref[h, rows, :] = (carry[h][2] / carry[h][1]).astype(o_ref.dtype)
        return 0

    lax.fori_loop(0, seq // blk, per_block, 0)


def attention(q, k, v, head_dim):
    n_heads, seq, width = q.shape
    blk = min(512, seq)
    return pl.pallas_call(
        functools.partial(attention_kernel, blk, head_dim ** -0.5),
        out_shape=jax.ShapeDtypeStruct((n_heads, seq, width), jnp.bfloat16),
        in_specs=[pl.BlockSpec(memory_space=pltpu.VMEM)] * 3,
        out_specs=pl.BlockSpec(memory_space=pltpu.VMEM),
        compiler_params=pltpu.CompilerParams(vmem_limit_bytes=48 * 2 ** 20),
        cost_estimate=pl.CostEstimate(flops=4 * n_heads * seq * seq * width, bytes_accessed=8 * n_heads * seq * width,
                                      transcendentals=n_heads * seq * seq // 2),
        name="attention",
    )(q, k, v)


def neighbours(tp):
    me = lax.axis_index("tp")
    core = lax.rem(me, 2)
    right = lax.rem(me + 2, tp)
    left = lax.rem(me + tp - 2, tp)
    sibling = me + 1 - 2 * core
    return right, left, sibling


def entry_barrier(peers):
    barrier = pltpu.get_barrier_semaphore()
    for peer in peers:
        pl.semaphore_signal(barrier, inc=1, device_id={"tp": peer}, device_id_type=MESH_IDS)
    pl.semaphore_wait(barrier, len(peers))


def remote(src, dst, send_sem, recv_sem, peer):
    return pltpu.make_async_remote_copy(src_ref=src, dst_ref=dst, send_sem=send_sem, recv_sem=recv_sem,
                                        device_id={"tp": peer}, device_id_type=MESH_IDS)


def mlp_kernel(tp, up_tile, down_tile, h_hbm, x_ref, wu_hbm, bu_ref, wd_hbm, bd_ref, out_ref,
               ag, part, rs, wu, wd, u_ref, load_sem, ag_send, ag_recv, push_send, push_recv,
               part_send, part_recv, rs_send, rs_recv):
    n = tp // 2
    half = ag.shape[3]
    d_model = ag.shape[4]
    ff = wu.shape[1]
    right, left, sibling = neighbours(tp)
    ahead = (right, left)

    loads = [pltpu.make_async_copy(h_hbm.at[pl.ds(d * half, half)], ag.at[0, d, 0], load_sem.at[d]) for d in range(2)]
    loads.append(pltpu.make_async_copy(wu_hbm, wu, load_sem.at[2]))
    loads.append(pltpu.make_async_copy(wd_hbm, wd, load_sem.at[3]))
    for copy in loads:
        copy.start()
    entry_barrier((right, left, sibling))

    def forward(s, d):
        return remote(ag.at[s, d, 0], ag.at[s + 1, d, 0], ag_send.at[s, d], ag_recv.at[s + 1, d], ahead[d])

    def push(s, d):
        return remote(ag.at[s, d, 0], ag.at[s, d, 1], push_send.at[s, d], push_recv.at[s, d], sibling)

    def give(s, d):
        return remote(ag.at[s, d, 1], part.at[s, d], part_send.at[s, d], part_recv.at[s, d], sibling)

    def reduce_send(s, d):
        return remote(part.at[s, d], rs.at[s, d], rs_send.at[s, d], rs_recv.at[s, d], ahead[d])

    for d in range(2):
        loads[d].wait()
        forward(0, d).start()
        push(0, d).start()
    loads[2].wait()
    loads[3].wait()

    def stage(i, _):
        s = lax.rem(i, n)
        last = i == n

        for d in range(2):
            @pl.when(jnp.logical_not(last))
            def _():
                forward(s - 1, d).wait_recv()

                @pl.when(i < n - 1)
                def _():
                    forward(s, d).start()

                push(s, d).start()

        for d in range(2):
            push(s, d).wait_recv()

        def up(t, _):
            cols = pl.ds(pl.multiple_of(t * up_tile, up_tile), up_tile)
            acc = jnp.dot(ag[s].reshape(4 * half, d_model), wu[:, cols], preferred_element_type=jnp.float32)
            u_ref[:, cols] = jax.nn.gelu(acc + bu_ref[:, cols].astype(jnp.float32), approximate=True).astype(jnp.bfloat16)
            return 0

        lax.fori_loop(0, ff // up_tile, up, 0)

        def down_sibling(t, _):
            cols = pl.ds(pl.multiple_of(t * down_tile, down_tile), down_tile)
            lhs = jnp.concatenate([u_ref[pl.ds(half, half), :], u_ref[pl.ds(3 * half, half), :]], axis=0)
            acc = jnp.dot(lhs, wd[:, cols], preferred_element_type=jnp.float32)
            for d in range(2):
                ag[s, d, 1, :, cols] = acc[d * half:(d + 1) * half].astype(jnp.bfloat16)
            return 0

        lax.fori_loop(0, d_model // down_tile, down_sibling, 0)
        for d in range(2):
            give(s, d).start()
        for d in range(2):
            give(s, d).wait_recv()

            @pl.when(i >= 2)
            def _():
                reduce_send(i - 1, d).wait_recv()

        def own_rows(t):
            cols = pl.ds(pl.multiple_of(t * down_tile, down_tile), down_tile)
            lhs = jnp.concatenate([u_ref[pl.ds(0, half), :], u_ref[pl.ds(2 * half, half), :]], axis=0)
            return cols, jnp.dot(lhs, wd[:, cols], preferred_element_type=jnp.float32)

        def add_terms(acc, d, cols, first):
            total = acc[d * half:(d + 1) * half] + part[s, d, :, cols].astype(jnp.float32)
            return total if first else total + rs[i - 1, d, :, cols].astype(jnp.float32)

        def down_first(t, _):
            cols, acc = own_rows(t)
            for d in range(2):
                part[s, d, :, cols] = add_terms(acc, d, cols, True).astype(jnp.bfloat16)
            return 0

        def down_middle(t, _):
            cols, acc = own_rows(t)
            for d in range(2):
                part[s, d, :, cols] = add_terms(acc, d, cols, False).astype(jnp.bfloat16)
            return 0

        def down_last(t, _):
            cols, acc = own_rows(t)
            bias = bd_ref[:, cols].astype(jnp.float32)
            for d in range(2):
                rows = pl.ds(d * half, half)
                total = add_terms(acc, d, cols, False) + bias
                out_ref[rows, cols] = (x_ref[rows, cols].astype(jnp.float32) + total).astype(jnp.bfloat16)
            return 0

        tiles = d_model // down_tile

        @pl.when(i == 1)
        def _():
            lax.fori_loop(0, tiles, down_first, 0)

        @pl.when(jnp.logical_and(i > 1, i < n))
        def _():
            lax.fori_loop(0, tiles, down_middle, 0)

        @pl.when(i < n)
        def _():
            for d in range(2):
                reduce_send(s, d).start()

        @pl.when(last)
        def _():
            lax.fori_loop(0, tiles, down_last, 0)

        return 0

    lax.fori_loop(1, n + 1, stage, 0)

    def drain(s, _):
        for d in range(2):
            push(s, d).wait_send()
            give(s, d).wait_send()

            @pl.when(s < n - 1)
            def _():
                forward(s, d).wait_send()

            @pl.when(s >= 1)
            def _():
                reduce_send(s, d).wait_send()
        return 0

    lax.fori_loop(0, n, drain, 0)


def mlp(tp, h, x, w_up, b_up, w_down, b_down):
    rows, d_model = h.shape
    ff = w_up.shape[1]
    n, half = tp // 2, rows // 2
    up_tile, down_tile = min(256, ff), min(512, d_model)
    vmem = pl.BlockSpec(memory_space=pltpu.VMEM)
    hbm = pl.BlockSpec(memory_space=pl.ANY)
    dma = pltpu.SemaphoreType.DMA
    return pl.pallas_call(
        functools.partial(mlp_kernel, tp, up_tile, down_tile),
        out_shape=jax.ShapeDtypeStruct((rows, d_model), jnp.bfloat16),
        in_specs=[hbm, vmem, hbm, vmem, hbm, vmem],
        out_specs=vmem,
        scratch_shapes=[
            pltpu.VMEM((n, 2, 2, half, d_model), jnp.bfloat16),
            pltpu.VMEM((n, 2, half, d_model), jnp.bfloat16),
            pltpu.VMEM((n, 2, half, d_model), jnp.bfloat16),
            pltpu.VMEM((d_model, ff), jnp.bfloat16),
            pltpu.VMEM((ff, d_model), jnp.bfloat16),
            pltpu.VMEM((4 * half, ff), jnp.bfloat16),
            dma((4,)),
        ] + [dma((n, 2))] * 8,
        compiler_params=pltpu.CompilerParams(collective_id=1, has_side_effects=True, vmem_limit_bytes=67043328),
        cost_estimate=pl.CostEstimate(flops=4 * tp * rows * d_model * ff, bytes_accessed=4 * d_model * ff, transcendentals=tp * rows * ff),
        name="mlp",
    )(h, x, w_up, b_up.reshape(1, ff), w_down, b_down.reshape(1, d_model))


def solution(mesh):
    tp = mesh.shape["tp"]

    def device_body(hidden, ln1_gain, ln1_bias, w_qkv, b_qkv, w_out, b_out, ln2_gain, ln2_bias, w_up, b_up, w_down, b_down):
        rows, d_model = hidden.shape[1], hidden.shape[2]
        n_heads, head_dim = w_qkv.shape[2], w_qkv.shape[3]
        x = hidden[0]
        normed = layer_norm(x, ln1_gain, ln1_bias)
        normed_all = lax.all_gather(normed, "tp", axis=0, tiled=True)
        pad = LANES - head_dim
        w_pad = jnp.pad(w_qkv, ((0, 0), (0, 0), (0, 0), (0, pad))).reshape(d_model, 3 * n_heads * LANES)
        b_pad = jnp.pad(b_qkv, ((0, 0), (0, 0), (0, pad))).reshape(3 * n_heads * LANES)
        qkv = (jnp.dot(normed_all, w_pad, preferred_element_type=jnp.float32) + b_pad.astype(jnp.float32)).astype(jnp.bfloat16)
        qkv = qkv.reshape(tp * rows, 3, n_heads, LANES).transpose(1, 2, 0, 3)
        context = attention(qkv[0], qkv[1], qkv[2], head_dim)
        context = context[:, :, :head_dim].transpose(1, 0, 2).reshape(tp, rows, n_heads * head_dim)
        received = lax.all_to_all(context, "tp", 0, 0, tiled=True)
        w_out_all = lax.all_gather(w_out.reshape(n_heads * head_dim, d_model), "tp", axis=0, tiled=True)
        ctx = received.transpose(1, 0, 2).reshape(rows, tp * n_heads * head_dim)
        attn = jnp.dot(ctx, w_out_all, preferred_element_type=jnp.float32)
        x1 = (x.astype(jnp.float32) + (attn + b_out.astype(jnp.float32))).astype(jnp.bfloat16)
        h2 = layer_norm(x1, ln2_gain, ln2_bias)
        return mlp(tp, h2, x1, w_up, b_up, w_down, b_down)[None]

    in_layout = (P("dp", "tp", None), P(), P(), P(None, None, "tp", None), P(None, "tp", None), P("tp", None, None), P(), P(), P(), P(None, "tp"), P("tp"), P("tp", None), P())
    return jax.shard_map(device_body, mesh=mesh, in_specs=in_layout, out_specs=P("dp", "tp", None), check_vma=False)
```

time: 1670 us -> 558 us (0.33)
  waiting for transfers between devices: 1390 us -> 169 us
  Pallas kernels: 0 us -> 297 us
  matrix products: 192 us -> 35.5 us
  other arithmetic: 54.5 us -> 8.23 us
  local copies, waits for them, and re-layouts: 0.06 us -> 29.7 us
    all_to_all x2 -> x1, waiting for transfers between devices: 1140 us -> 32.7 us  [device_body(): received = lax.all_to_all(context, 'tp', 0, 0, tiled=True)]
    pallas_call x0 -> x2, Pallas kernels: none -> 297 us  [the longest x1 251 us: mlp(): pl.pallas_call(functools.partial(mlp_kernel, tp, up_tile, down_tile), out...]
    all_gather x2, waiting for transfers between devices: 256 us -> 135 us  [the longest x1 131 us: device_body(): normed_all = lax.all_gather(normed, 'tp', axis=0, tiled=True)]
    dot_general x4 -> x2, matrix products: 107 us -> 35.5 us  [the longest x1 25.8 us: device_body(): jnp.dot(normed_all, w_pad, preferred_element_type=jnp.float32)]
    sub x1 -> x0, matrix products: 67.5 us -> none  [causal_attention(): exp_vals = jnp.exp(logits - row_max)]
    reduce_sum x2 -> x0, other arithmetic: 28 us -> none  [scatter_sum(): return jnp.sum(received.astype(jnp.float32), axis=1)]
    unnamed x1 -> x0, matrix products: 18.2 us -> none
  transfers between devices with their start and end apart: 4 -> 3, of which waited for: 4 -> 3; matrix products, arithmetic and copies ran while one was open for 1% -> 9% of each run, Pallas kernels for 0% -> 8%
where the time goes in v1:
time: 558 us
  Pallas kernels  297 us (53%)
  waiting for transfers between devices  169 us (30%)
  matrix products  35.5 us (6%)
  local copies, waits for them, and re-layouts  29.7 us (5%)
  between operations  13.6 us (2%)
  other arithmetic  8.23 us (1%)
    pallas_call x1, Pallas kernels, mlp(): pl.pallas_call(functools.partial(mlp_kernel, tp, up_tile, down_tile), out...  251 us
    all_gather x1, waiting for transfers between devices, device_body(): normed_all = lax.all_gather(normed, 'tp', axis=0, tiled=True)  131 us
    pallas_call x1, Pallas kernels, attention(): pl.pallas_call(functools.partial(attention_kernel, blk, head_dim ** (-0.5...  45.5 us
    all_to_all x1, waiting for transfers between devices, device_body(): received = lax.all_to_all(context, 'tp', 0, 0, tiled=True)  32.7 us
    dot_general x1, matrix products, device_body(): jnp.dot(normed_all, w_pad, preferred_element_type=jnp.float32)  25.8 us
  transfers between devices with their start and end apart: 3, of which 3 were waited for; matrix products, arithmetic and copies ran while one was open for 9% of the time, Pallas kernels for 8%

profile of v1, /device:TPU:21, one launch (start us, length us, event | category | flops | bytes accessed | tf_op | source)
XLA Modules:
  0.0 557.5 jit_solution(4232799692791648120)
XLA Ops:
  6.5 0.0 copy-start
  6.5 0.0 copy-start.3
  6.6 0.0 copy-start.2
  6.6 0.0 all-gather.3.cloned.1.call-start
  6.6 1.8 convert_reduce_fusion.1
  8.4 2.0 fusion.11
  10.3 0.0 copy-start.9
  10.4 0.0 copy-done
  10.4 0.0 copy-done.3
  10.4 0.0 copy-done.2
  10.4 1.9 fusion.14
  12.3 0.1 all-gather.3.cloned.1.call-update
  12.4 0.1 all-gather.5.cloned.1.call-start
  12.5 0.7 all-gather.5.cloned.1.call-update
  13.2 0.0 copy-done.9
  13.2 4.8 pad.8
  18.0 131.0 %all-gather.3.cloned.1.call-done = bf16[4096,3072]{1,0:T(8,128)(2,1)} async-done(((bf16[256,3072]{1,0:T(8,128)(2,1)}), bf16[4096,3072]{1,0:T(8,128)(2,1)}) %all-gather.3.cloned.1.call-update) | async-done | bytes 25165840 | tf_op jit(solution)/shard_map/all_gather | solution.py:285
  149.1 25.8 %add_convert_fusion = bf16[4096,768]{0,1:T(8,128)(2,1)} fusion(bf16[4096,3072]{1,0:T(8,128)(2,1)} %all-gather.3.cloned.1.call-done, bf16[3072,768]{0,1:T(8,128)(2,1)} %bitcast.52, f32[768]{0:T(1024)S(1)} %reshape.66), kind=kOutput, calls=%fused_computation | convolution fusion | flops 19333644288 | bytes 36178944 | tf_op jit(solution)/shard_map/dot_general | solution.py:289
  174.8 8.7 %copy.17 = bf16[4096,3,2,128]{3,0,2,1:T(8,128)(2,1)} copy(bf16[4096,3,2,128]{0,3,2,1:T(8,128)(2,1)} %bitcast.48) | data formatting | bytes 12582912 | tf_op jit(solution)/shard_map/reshape | solution.py:290
  183.5 5.3 slice_bitcast_fusion.1
  188.8 45.5 %attention.1 = bf16[2,4096,128]{2,1,0:T(8,128)(2,1)S(1)} custom-call(bf16[2,4096,128]{2,1,0:T(8,128)(2,1)S(1)} %get-tuple-element.7.q_ref, bf16[2,4096,128]{2,1,0:T(8,128)(2,1)} %get-tuple-element.6.k_ref, bf16[2,4096,128]{2,1,0:T(8,128)(2,1)} %get-tuple-element.5.v_ref), custom_call_target="tpu_custom_call" | custom-call | flops 17179869184 | bytes 8388608 | tf_op jit(solution)/shard_map/attention/pallas_call | solution.py:66
  234.3 1.5 slice_bitcast_fusion
  235.7 2.9 copy.18
  238.6 0.4 copy.21
  239.1 0.0 copy-start.6
  239.1 0.0 copy-start.7
  239.1 0.0 copy-start.8
  239.1 1.7 copy.19
  240.8 4.7 all-to-all-start
  245.5 0.0 copy-done.6
  245.6 0.0 copy-done.7
  245.6 0.6 reshape.65.bd_ref
  246.2 0.0 copy-done.8
  246.2 0.6 reshape.64.bu_ref
  246.8 4.4 all-gather.5.cloned.1.call-done
  251.1 32.7 %all-to-all-done = bf16[16,256,192]{1,2,0:T(8,128)(2,1)S(1)} async-done(((bf16[16,256,192]{1,2,0:T(8,128)(2,1)}), bf16[16,256,192]{1,2,0:T(8,128)(2,1)S(1)}, u32[]{:S(2)}, u32[]{:S(2)}) %all-to-all-start) | async-done | bytes 1572896 | tf_op jit(solution)/shard_map/all_to_all | solution.py:293
  283.8 0.0 copy-start.4
  283.8 0.0 copy-start.5
  283.8 9.7 %convert_reduce_fusion = (f32[256]{0:T(256)S(1)}, bf16[256,3072]{1,0:T(8,128)(2,1)S(1)}) fusion(f32[3072]{0:T(1024)S(1)} %convert_element_type.45, bf16[256,3072]{0,1:T(8,128)(2,1)S(1)} %bitcast.49, bf16[3072,3072]{1,0:T(8,128)(2,1)} %all-gather.5.cloned.1.call-done, bf16[1,256,3072]{2,1,0:T(8,128)(2,1)S(1)} %copy-done), kind=kOutput, calls=%fused_computation.4 | convolution fusion | flops 4836556800 | bytes 23606272 | tf_op jit(solution)/shard_map/dot_general | solution.py:296
  293.6 0.0 copy-start.1
  293.6 0.6 fusion.7
  294.2 0.6 copy-done.1
  294.7 0.0 copy-done.4
  294.7 0.0 copy-done.5
  294.7 1.9 fusion.10.h_hbm
  296.7 251.4 %mlp.1 = bf16[256,3072]{1,0:T(8,128)(2,1)} custom-call(bf16[256,3072]{1,0:T(8,128)(2,1)} %fusion.10.h_hbm, bf16[256,3072]{1,0:T(8,128)(2,1)} %copy-done.1, bf16[3072,768]{1,0:T(8,128)(2,1)} %wu_hbm.1, bf16[1,768]{1,0:T(2,128)(2,1)} %reshape.64.bu_ref, bf16[768,3072]{1,0:T(8,128)(2,1)} %wd_hbm.1, bf16[1,3072]{1,0:T(2,128)(2,1)} %reshape.65.bd_ref), custom_call_target="tpu_custom_call" | custom-call | flops 38654705664 | bytes 9437184 | tf_op jit(solution)/shard_map/mlp/pallas_call | solution.py:257
  548.0 2.7 copy.24
  (7 shorter events, 0.0 us)
Async XLA Ops:
  6.5 3.8 copy-start
  6.5 3.8 copy-start.3
  6.6 3.8 copy-start.2
  6.6 142.5 %all-gather.3.cloned.1.call-start = ((), (), s32[]{:S(2)}) async-start(), calls=%async_computation.1 | async-start | bytes 26738688 | tf_op jit(solution)/shard_map/all_gather | solution.py:285
  10.3 2.9 copy-start.9
  12.4 238.8 %all-gather.5.cloned.1.call-start = ((), (), s32[]{:S(2)}) async-start(), calls=%async_computation.2 | async-start | bytes 20054016 | tf_op jit(solution)/shard_map/all_gather | solution.py:294
  239.1 6.5 %copy-start.6 = (bf16[3072]{0:T(1024)(128)(2,1)S(1)}, bf16[3072]{0:T(1024)(128)(2,1)}, u32[]{:S(2)}) copy-start(bf16[3072]{0:T(1024)(128)(2,1)} %param.19) | copy-start | bytes 18436
  239.1 6.5 %copy-start.7 = (bf16[3072]{0:T(1024)(128)(2,1)S(1)}, bf16[3072]{0:T(1024)(128)(2,1)}, u32[]{:S(2)}) copy-start(bf16[3072]{0:T(1024)(128)(2,1)} %param.25) | copy-start | bytes 18436
  239.1 7.1 %copy-start.8 = (bf16[768]{0:T(1024)(128)(2,1)S(1)}, bf16[768]{0:T(1024)(128)(2,1)}, u32[]{:S(2)}) copy-start(bf16[768]{0:T(1024)(128)(2,1)} %param.23) | copy-start | bytes 4612
  240.8 43.0 %all-to-all-start = ((bf16[16,256,192]{1,2,0:T(8,128)(2,1)}), bf16[16,256,192]{1,2,0:T(8,128)(2,1)S(1)}, u32[]{:S(2)}, u32[]{:S(2)}) async-start(bf16[16,256,192]{1,2,0:T(8,128)(2,1)} %copy.19), calls=%async_computation | async-start | bytes 3145728 | tf_op jit(solution)/shard_map/all_to_all | solution.py:293
  283.8 10.9 %copy-start.4 = (f32[3072]{0:T(1024)S(1)}, f32[3072]{0:T(1024)}, u32[]{:S(2)}) copy-start(f32[3072]{0:T(1024)} %param.21) | copy-start | bytes 36868
  283.8 10.9 %copy-start.5 = (f32[3072]{0:T(1024)S(1)}, f32[3072]{0:T(1024)}, u32[]{:S(2)}) copy-start(f32[3072]{0:T(1024)} %param.20) | copy-start | bytes 36868
  293.6 1.1 copy-start.1
Sparse Core Ops, SparseCore 0:
  12.5 136.5 all-gather.2
  150.7 100.4 all-gather.4

commit v2 on v1

--- a/solution.py
+++ b/solution.py
@@ -19,60 +19,6 @@
     centered = as_f32 - row_mean
     variance = jnp.mean(centered * centered, axis=-1, keepdims=True)
     return (centered * lax.rsqrt(variance + LN_EPS) * gain_vec + shift_vec).astype(jnp.bfloat16)
-
-
-def attention_kernel(blk, scale, q_ref, k_ref, v_ref, o_ref):
-    n_heads, seq, width = q_ref.shape
-    factor = scale * math.log2(math.e)
-    row = lax.broadcasted_iota(jnp.int32, (blk, blk), 0)
-    col = lax.broadcasted_iota(jnp.int32, (blk, blk), 1)
-
-    def block(queries, j, carry, masked):
-        out = []
-        for h in range(n_heads):
-            m, l, acc = carry[h]
-            rows = pl.ds(pl.multiple_of(j * blk, blk), blk)
-            s = lax.dot_general(queries[h], k_ref[h, rows, :], (((1,), (1,)), ((), ())),
-                                preferred_element_type=jnp.float32)
-            if masked:
-                s = jnp.where(row >= col, s, -1e30)
-            m_new = jnp.maximum(m, jnp.max(s, axis=-1, keepdims=True))
-            p = jnp.exp2((s - m_new) * factor)
-            alpha = jnp.exp2((m - m_new) * factor)
-            l = l * alpha + jnp.sum(p, axis=-1, keepdims=True)
-            acc = acc * alpha + jnp.dot(p.astype(jnp.bfloat16), v_ref[h, rows, :],
-                                        preferred_element_type=jnp.float32)
-            out.append((m_new, l, acc))
-        return tuple(out)
-
-    def per_block(i, _):
-        rows = pl.ds(pl.multiple_of(i * blk, blk), blk)
-        queries = [q_ref[h, rows, :] for h in range(n_heads)]
-        init = tuple(
-            (jnp.full((blk, 1), -1e30, jnp.float32), jnp.zeros((blk, 1), jnp.float32),
-             jnp.zeros((blk, width), jnp.float32)) for _ in range(n_heads))
-        carry = block(queries, i, init, True)
-        carry = lax.fori_loop(0, i, lambda j, c: block(queries, j, c, False), carry)
-        for h in range(n_heads):
-            o_ref[h, rows, :] = (carry[h][2] / carry[h][1]).astype(o_ref.dtype)
-        return 0
-
-    lax.fori_loop(0, seq // blk, per_block, 0)
-
-
-def attention(q, k, v, head_dim):
-    n_heads, seq, width = q.shape
-    blk = min(512, seq)
-    return pl.pallas_call(
-        functools.partial(attention_kernel, blk, head_dim ** -0.5),
-        out_shape=jax.ShapeDtypeStruct((n_heads, seq, width), jnp.bfloat16),
-        in_specs=[pl.BlockSpec(memory_space=pltpu.VMEM)] * 3,
-        out_specs=pl.BlockSpec(memory_space=pltpu.VMEM),
-        compiler_params=pltpu.CompilerParams(vmem_limit_bytes=48 * 2 ** 20),
-        cost_estimate=pl.CostEstimate(flops=4 * n_heads * seq * seq * width, bytes_accessed=8 * n_heads * seq * width,
-                                      transcendentals=n_heads * seq * seq // 2),
-        name="attention",
-    )(q, k, v)
 
 
 def neighbours(tp):
@@ -94,6 +40,196 @@
 def remote(src, dst, send_sem, recv_sem, peer):
     return pltpu.make_async_remote_copy(src_ref=src, dst_ref=dst, send_sem=send_sem, recv_sem=recv_sem,
                                         device_id={"tp": peer}, device_id_type=MESH_IDS)
+
+
+def attend_kernel(tp, head_dim, x_ref, g_ref, be_ref, w_hbm, b_ref, out_ref,
+                  ag, wq, qt_ref, k_ref, vt_ref, pack, got, load_sem, ag_send, ag_recv, push_send, push_recv,
+                  ctx_send, ctx_recv):
+    n = tp // 2
+    half = ag.shape[3]
+    rows_own = 2 * half
+    d_model = ag.shape[4]
+    n_heads = qt_ref.shape[0]
+    blk = 2 * rows_own
+    me = lax.axis_index("tp")
+    core = lax.rem(me, 2)
+    chip = me // 2
+    right, left, sibling = neighbours(tp)
+    ahead = (right, left)
+
+    load = pltpu.make_async_copy(w_hbm, wq, load_sem)
+    load.start()
+    entry_barrier([lax.rem(me + k, tp) for k in range(1, tp)])
+
+    def forward(s, d):
+        return remote(ag.at[s, d, 0], ag.at[s + 1, d, 0], ag_send.at[s, d], ag_recv.at[s + 1, d], ahead[d])
+
+    def push(s, d):
+        return remote(ag.at[s, d, 0], ag.at[s, d, 1], push_send.at[s, d], push_recv.at[s, d], sibling)
+
+    ln_rows = 16
+    for d in range(2):
+        def norm(t, _):
+            at = pl.multiple_of(t * ln_rows, ln_rows)
+            rows = x_ref[pl.ds(d * half + at, ln_rows), :]
+            ag[0, d, 0, pl.ds(at, ln_rows), :] = layer_norm(rows, g_ref[...], be_ref[...])
+            return 0
+
+        lax.fori_loop(0, half // ln_rows, norm, 0)
+        forward(0, d).start()
+        push(0, d).start()
+    load.wait()
+
+    def stage(s, _):
+        @pl.when(s > 0)
+        def _():
+            for d in range(2):
+                forward(s - 1, d).wait_recv()
+
+                @pl.when(s < n - 1)
+                def _():
+                    forward(s, d).start()
+
+                push(s, d).start()
+
+        for d in range(2):
+            push(s, d).wait_recv()
+
+        source = (lax.rem(chip + n - s, n), lax.rem(chip + s, n))
+        starts = [pl.multiple_of((source[d] * 2 + (core if idx == 0 else 1 - core)) * rows_own + d * half, half)
+                  for d in range(2) for idx in range(2)]
+        width = n_heads * LANES
+        for part in range(3):
+            cols = slice(part * width, (part + 1) * width)
+            acc = jnp.dot(ag[s].reshape(4 * half, d_model), wq[:, cols], preferred_element_type=jnp.float32)
+            acc = acc + b_ref[:, cols].astype(jnp.float32)
+            for h in range(n_heads):
+                for p in range(4):
+                    tile = acc[p * half:(p + 1) * half, h * LANES:(h + 1) * LANES]
+                    if part == 1:
+                        k_ref[h, pl.ds(starts[p], half), :] = tile.astype(jnp.bfloat16)
+                    else:
+                        (qt_ref if part == 0 else vt_ref)[h, :, pl.ds(starts[p], half)] = tile.T.astype(jnp.bfloat16)
+        return 0
+
+    lax.fori_loop(0, n, stage, 0)
+
+    factor = head_dim ** -0.5 * math.log2(math.e)
+
+    def block(qt, j, carry, masked):
+        out = []
+        rows = pl.ds(pl.multiple_of(j * blk, blk), blk)
+        for h in range(n_heads):
+            m, l, acc = carry[h]
+            s = jnp.dot(k_ref[h, rows, :], qt[h], preferred_element_type=jnp.float32)
+            if masked:
+                key = lax.broadcasted_iota(jnp.int32, (blk, blk), 0)
+                query = lax.broadcasted_iota(jnp.int32, (blk, blk), 1)
+                s = jnp.where(query >= key, s, -1e30)
+            m_new = jnp.maximum(m, jnp.max(s, axis=0, keepdims=True))
+            p = jnp.exp2((s - m_new) * factor)
+            alpha = jnp.exp2((m - m_new) * factor)
+            l = l * alpha + jnp.sum(p, axis=0, keepdims=True)
+            acc = acc * alpha + jnp.dot(vt_ref[h, :head_dim, rows], p.astype(jnp.bfloat16), preferred_element_type=jnp.float32)
+            out.append((m_new, l, acc))
+        return tuple(out)
+
+    def send_ctx(dest):
+        return remote(pack.at[dest], got.at[me], ctx_send.at[dest], ctx_recv.at[me], dest)
+
+    def take_ctx(source):
+        return remote(pack.at[source], got.at[source], ctx_send.at[source], ctx_recv.at[source], source)
+
+    def per_chip(t, _):
+        step = jnp.where(lax.rem(t, 2) == 1, n // 2 - (t + 1) // 2, n // 2 + t // 2)
+        i = lax.rem(chip + step, n)
+        cols = pl.ds(pl.multiple_of(i * blk, blk), blk)
+        qt = [qt_ref[h, :, cols] for h in range(n_heads)]
+        init = tuple((jnp.full((1, blk), -1e30, jnp.float32), jnp.zeros((1, blk), jnp.float32),
+                      jnp.zeros((head_dim, blk), jnp.float32)) for _ in range(n_heads))
+        carry = block(qt, i, init, True)
+        carry = lax.fori_loop(0, i, lambda j, c: block(qt, j, c, False), carry)
+        full = jnp.concatenate([acc / l for _, l, acc in carry], axis=0)
+        for e in range(2):
+            dest = 2 * i + e
+            mine = full[:, e * rows_own:(e + 1) * rows_own]
+            pack[dest, :rows_own, :] = mine[:LANES].T.astype(jnp.bfloat16)
+            tail = jnp.concatenate([mine[LANES:, :half], mine[LANES:, half:]], axis=0)
+            pack[dest, rows_own:, :] = tail.T.astype(jnp.bfloat16)
+
+            @pl.when(dest != me)
+            def _():
+                send_ctx(dest).start()
+        return 0
+
+    lax.fori_loop(0, n, per_chip, 0)
+    got[me] = pack[me]
+
+    def take(t, _):
+        @pl.when(t != me)
+        def _():
+            take_ctx(t).wait_recv()
+        return 0
+
+    lax.fori_loop(0, tp, take, 0)
+    rest = LANES // 2
+    for c in range(n):
+        first, second = got[2 * c], got[2 * c + 1]
+        tails = [jnp.concatenate([g[rows_own:, :rest], g[rows_own:, rest:]], axis=0) for g in (first, second)]
+        at = c * 3 * LANES
+        out_ref[:, at:at + LANES] = first[:rows_own]
+        out_ref[:, at + LANES:at + 2 * LANES] = jnp.concatenate([tails[0], second[:rows_own, :rest]], axis=1)
+        out_ref[:, at + 2 * LANES:at + 3 * LANES] = jnp.concatenate([second[:rows_own, rest:], tails[1]], axis=1)
+
+    def drain(s, _):
+        for d in range(2):
+            push(s, d).wait_send()
+
+            @pl.when(s < n - 1)
+            def _():
+                forward(s, d).wait_send()
+        for e in range(2):
+            @pl.when(2 * s + e != me)
+            def _():
+                send_ctx(2 * s + e).wait_send()
+        return 0
+
+    lax.fori_loop(0, n, drain, 0)
+
+
+def attend(tp, x, gain, shift, w_qkv, b_qkv):
+    rows, d_model = x.shape
+    n_heads, head_dim = w_qkv.shape[2], w_qkv.shape[3]
+    assert n_heads == 2 and 2 * n_heads * head_dim == 3 * LANES
+    n, half = tp // 2, rows // 2
+    seq = tp * rows
+    width = 3 * n_heads * LANES
+    pad = LANES - head_dim
+    w_pad = jnp.pad(w_qkv, ((0, 0), (0, 0), (0, 0), (0, pad))).reshape(d_model, width)
+    b_pad = jnp.pad(b_qkv, ((0, 0), (0, 0), (0, pad))).reshape(1, width)
+    vmem = pl.BlockSpec(memory_space=pltpu.VMEM)
+    hbm = pl.BlockSpec(memory_space=pl.ANY)
+    dma = pltpu.SemaphoreType.DMA
+    return pl.pallas_call(
+        functools.partial(attend_kernel, tp, head_dim),
+        out_shape=jax.ShapeDtypeStruct((rows, tp * n_heads * head_dim), jnp.bfloat16),
+        in_specs=[vmem, vmem, vmem, hbm, vmem],
+        out_specs=vmem,
+        scratch_shapes=[
+            pltpu.VMEM((n, 2, 2, half, d_model), jnp.bfloat16),
+            pltpu.VMEM((d_model, width), jnp.bfloat16),
+            pltpu.VMEM((n_heads, LANES, seq), jnp.bfloat16),
+            pltpu.VMEM((n_heads, seq, LANES), jnp.bfloat16),
+            pltpu.VMEM((n_heads, LANES, seq), jnp.bfloat16),
+            pltpu.VMEM((tp, 3 * half, LANES), jnp.bfloat16),
+            pltpu.VMEM((tp, 3 * half, LANES), jnp.bfloat16),
+            dma,
+        ] + [dma((n, 2))] * 4 + [dma((tp,))] * 2,
+        compiler_params=pltpu.CompilerParams(collective_id=2, has_side_effects=True, vmem_limit_bytes=67043328),
+        cost_estimate=pl.CostEstimate(flops=150 * 10 ** 9, bytes_accessed=2 * d_model * width,
+                                      transcendentals=n_heads * seq * seq // 2),
+        name="attend",
+    )(x, gain.reshape(1, d_model), shift.reshape(1, d_model), w_pad, b_pad)
 
 
 def mlp_kernel(tp, up_tile, down_tile, h_hbm, x_ref, wu_hbm, bu_ref, wd_hbm, bd_ref, out_ref,
@@ -275,25 +411,19 @@
 
 
 def solution(mesh):
-    tp = mesh.shape["tp"]
+    tp, dp = mesh.shape["tp"], mesh.shape["dp"]
 
     def device_body(hidden, ln1_gain, ln1_bias, w_qkv, b_qkv, w_out, b_out, ln2_gain, ln2_bias, w_up, b_up, w_down, b_down):
         rows, d_model = hidden.shape[1], hidden.shape[2]
         n_heads, head_dim = w_qkv.shape[2], w_qkv.shape[3]
         x = hidden[0]
-        normed = layer_norm(x, ln1_gain, ln1_bias)
-        normed_all = lax.all_gather(normed, "tp", axis=0, tiled=True)
-        pad = LANES - head_dim
-        w_pad = jnp.pad(w_qkv, ((0, 0), (0, 0), (0, 0), (0, pad))).reshape(d_model, 3 * n_heads * LANES)
-        b_pad = jnp.pad(b_qkv, ((0, 0), (0, 0), (0, pad))).reshape(3 * n_heads * LANES)
-        qkv = (jnp.dot(normed_all, w_pad, preferred_element_type=jnp.float32) + b_pad.astype(jnp.float32)).astype(jnp.bfloat16)
-        qkv = qkv.reshape(tp * rows, 3, n_heads, LANES).transpose(1, 2, 0, 3)
-        context = attention(qkv[0], qkv[1], qkv[2], head_dim)
-        context = context[:, :, :head_dim].transpose(1, 0, 2).reshape(tp, rows, n_heads * head_dim)
-        received = lax.all_to_all(context, "tp", 0, 0, tiled=True)
-        w_out_all = lax.all_gather(w_out.reshape(n_heads * head_dim, d_model), "tp", axis=0, tiled=True)
-        ctx = received.transpose(1, 0, 2).reshape(rows, tp * n_heads * head_dim)
-        attn = jnp.dot(ctx, w_out_all, preferred_element_type=jnp.float32)
+        share = n_heads * head_dim // dp
+        w_mine = lax.dynamic_slice_in_dim(w_out.reshape(n_heads * head_dim, d_model), lax.axis_index("dp") * share, share, 0)
+        w_share = lax.all_gather(w_mine, "tp", axis=0)
+        w_all = lax.all_gather(w_share, "dp", axis=0)
+        ctx = attend(tp, x, ln1_gain, ln1_bias, w_qkv, b_qkv)
+        ctx = ctx.reshape(rows, tp, dp, share)
+        attn = jnp.einsum("qtjr,jtre->qe", ctx, w_all, preferred_element_type=jnp.float32)
         x1 = (x.astype(jnp.float32) + (attn + b_out.astype(jnp.float32))).astype(jnp.bfloat16)
         h2 = layer_norm(x1, ln2_gain, ln2_bias)
         return mlp(tp, h2, x1, w_up, b_up, w_down, b_down)[None]

time: 558 us -> 531 us (0.952)
  Pallas kernels: 297 us -> 441 us
  waiting for transfers between devices: 169 us -> 44.6 us
  matrix products: 35.5 us -> 9.75 us
  local copies, waits for them, and re-layouts: 29.7 us -> 18.2 us
  other arithmetic: 8.23 us -> 2.49 us
    pallas_call x1, Pallas kernels: 45.5 us -> 190 us  [attend(): pl.pallas_call(functools.partial(attend_kernel, tp, head_dim), out_shape=...]
    all_gather x2, waiting for transfers between devices: 135 us -> 44.5 us  [the longest x1 44.5 us: device_body(): w_share = lax.all_gather(w_mine, 'tp', axis=0)]
    all_to_all x1 -> x0, waiting for transfers between devices: 32.7 us -> none  [device_body(): received = lax.all_to_all(context, 'tp', 0, 0, tiled=True)]
    dot_general x2 -> x1, matrix products: 35.5 us -> 9.75 us  [device_body(): jnp.einsum('qtjr,jtre->qe', ctx, w_all, preferred_element_type=jnp.float32)]
  transfers between devices with their start and end apart: 3 -> 2, of which waited for: 3 -> 1; matrix products, arithmetic and copies ran while one was open for 9% -> 2% of each run, Pallas kernels for 8% -> 36%
where the time goes in v2:
time: 531 us; the launch traced here: 530 us
  Pallas kernels  441 us (83%)
  waiting for transfers between devices  44.6 us (8%)
  local copies, waits for them, and re-layouts  18.2 us (3%)
  between operations  13.6 us (3%)
  matrix products  9.75 us (2%)
    pallas_call x1, Pallas kernels, mlp(): pl.pallas_call(functools.partial(mlp_kernel, tp, up_tile, down_tile), out...  252 us
    pallas_call x1, Pallas kernels, attend(): pl.pallas_call(functools.partial(attend_kernel, tp, head_dim), out_shape=...  190 us
    all_gather x1, waiting for transfers between devices, device_body(): w_share = lax.all_gather(w_mine, 'tp', axis=0)  44.5 us
  transfers between devices with their start and end apart: 2, of which 1 were waited for; matrix products, arithmetic and copies ran while one was open for 2% of the time, Pallas kernels for 36%

profile of v2, /device:TPU:21, one launch (start us, length us, event | category | flops | bytes accessed | tf_op | source)
XLA Modules:
  0.0 530.0 jit_solution(15123238085465386304)
XLA Ops:
  6.5 0.0 copy-start.1
  6.5 0.0 all-gather.5.cloned.1.call-start
  6.6 1.8 constant_dynamic-slice_fusion
  8.4 0.1 all-gather.5.cloned.1.call-update
  8.5 0.1 all-gather.7.cloned.1.call-start
  8.5 44.5 %all-gather.5.cloned.1.call-done = bf16[768,3072]{1,0:T(8,128)(2,1)} async-done(((bf16[48,3072]{1,0:T(8,128)(2,1)}), bf16[768,3072]{1,0:T(8,128)(2,1)}) %all-gather.5.cloned.1.call-update) | async-done | bytes 4718608 | tf_op jit(solution)/shard_map/all_gather | solution.py:422
  53.0 0.1 all-gather.7.cloned.1.call-update
  53.1 0.0 copy-done.1
  53.1 2.7 pad.8
  55.8 0.0 copy-start.8
  55.8 6.7 %copy.23.w_hbm = bf16[3072,768]{1,0:T(8,128)(2,1)} copy(bf16[3072,768]{0,1:T(8,128)(2,1)} %bitcast.22) | data formatting | bytes 9437184 | tf_op jit(solution)/shard_map/reshape | solution.py:208
  62.5 0.0 copy-done.8
  62.6 0.6 reshape.42.b_ref
  63.1 189.6 %attend.1 = bf16[256,3072]{1,0:T(8,128)(2,1)} custom-call(bf16[256,3072]{1,0:T(8,128)(2,1)} %bitcast.25, f32[1,3072]{1,0:T(1,128)} %bitcast.28, f32[1,3072]{1,0:T(1,128)} %bitcast.29, bf16[3072,768]{1,0:T(8,128)(2,1)} %copy.23.w_hbm, bf16[1,768]{1,0:T(2,128)(2,1)} %reshape.42.b_ref), custom_call_target="tpu_custom_call" | custom-call | flops 149999992832 | bytes 4718592 | tf_op jit(solution)/shard_map/attend/pallas_call | solution.py:213
  252.7 0.0 copy-start.5
  252.7 0.0 copy-start.6
  252.7 0.0 copy-start.7
  252.8 0.0 copy-start.2
  252.8 1.8 copy.20
  254.6 0.0 copy-done.5
  254.6 0.0 copy-done.6
  254.6 0.6 reshape.46.bd_ref
  255.3 0.0 copy-done.7
  255.3 0.6 reshape.45.bu_ref
  255.8 0.0 all-gather.7.cloned.1.call-done
  255.8 0.0 copy-done.2
  255.9 0.0 copy-start.3
  255.9 0.0 copy-start.4
  255.9 9.7 %convert_reduce_fusion = (f32[256]{0:T(256)S(1)}, bf16[256,3072]{1,0:T(8,128)(2,1)S(1)}) fusion(f32[3072]{0:T(1024)S(1)} %convert_element_type.20, bf16[4,16,48,3072]{3,2,1,0:T(8,128)(2,1)} %bitcast.21, bf16[256,16,4,48]{0,3,2,1:T(8,128)(2,1)S(1)} %bitcast.23, bf16[1,256,3072]{2,1,0:T(8,128)(2,1)S(1)} %copy-done.2), kind=kOutput, calls=%fused_computation.4 | convolution fusion | flops 4836556800 | bytes 23606272 | tf_op jit(solution)/shard_map/qtjr,jtre->qe/dot_general | solution.py:426
  265.6 0.0 copy-start
  265.6 0.6 fusion.5
  266.2 0.6 copy-done
  266.8 0.0 copy-done.3
  266.8 0.0 copy-done.4
  266.8 1.9 fusion.8.h_hbm
  268.7 251.8 %mlp.1 = bf16[256,3072]{1,0:T(8,128)(2,1)} custom-call(bf16[256,3072]{1,0:T(8,128)(2,1)} %fusion.8.h_hbm, bf16[256,3072]{1,0:T(8,128)(2,1)} %copy-done, bf16[3072,768]{1,0:T(8,128)(2,1)} %wu_hbm.1, bf16[1,768]{1,0:T(2,128)(2,1)} %reshape.45.bu_ref, bf16[768,3072]{1,0:T(8,128)(2,1)} %wd_hbm.1, bf16[1,3072]{1,0:T(2,128)(2,1)} %reshape.46.bd_ref), custom_call_target="tpu_custom_call" | custom-call | flops 38654705664 | bytes 9437184 | tf_op jit(solution)/shard_map/mlp/pallas_call | solution.py:393
  520.5 2.7 copy.29
  (4 shorter events, 0.0 us)
Async XLA Ops:
  6.5 46.6 %copy-start.1 = (bf16[3072,3,2,96]{0,3,2,1:T(8,128)(2,1)S(1)}, bf16[3072,3,2,96]{0,3,2,1:T(8,128)(2,1)}, u32[]{:S(2)}) copy-start(bf16[3072,3,2,96]{0,3,2,1:T(8,128)(2,1)} %param.16) | copy-start | bytes 10616836
  6.5 46.5 %all-gather.5.cloned.1.call-start = ((), (), s32[]{:S(2)}) async-start(), calls=%async_computation | async-start | bytes 5013504 | tf_op jit(solution)/shard_map/all_gather | solution.py:422
  8.5 247.4 %all-gather.7.cloned.1.call-start = ((), (), s32[]{:S(2)}) async-start(), calls=%async_computation.1 | async-start | bytes 23592960 | tf_op jit(solution)/shard_map/all_gather | solution.py:423
  55.8 6.7 %copy-start.8 = (bf16[3,2,96]{2,1,0:T(2,128)(2,1)S(1)}, bf16[3,2,96]{2,1,0:T(2,128)(2,1)}, u32[]{:S(2)}) copy-start(bf16[3,2,96]{2,1,0:T(2,128)(2,1)} %param.17) | copy-start | bytes 3460
  252.7 1.9 copy-start.5
  252.7 1.9 copy-start.6
  252.7 2.5 copy-start.7
  252.8 3.1 copy-start.2
  255.9 10.9 %copy-start.3 = (f32[3072]{0:T(1024)S(1)}, f32[3072]{0:T(1024)}, u32[]{:S(2)}) copy-start(f32[3072]{0:T(1024)} %param.21) | copy-start | bytes 36868
  255.9 10.9 %copy-start.4 = (f32[3072]{0:T(1024)S(1)}, f32[3072]{0:T(1024)}, u32[]{:S(2)}) copy-start(f32[3072]{0:T(1024)} %param.20) | copy-start | bytes 36868
  265.6 1.2 copy-start
Sparse Core Ops, SparseCore 0:
  9.0 44.0 all-gather.4
  55.0 178.4 all-gather.6
